TPU v7x, 32 devices: a whole 2x2x4 slice. The times are simulated.
32 devices in a mesh: gx: 4 (over x, core), gy: 8 (over z, y).
Axes of the slice: x: 2, y: 2, z: 4, core: 2. Of those that a mesh axis runs over, the one named last changes fastest.
Arguments:
- atm_fields: bfloat16 [196608, 128], P(('gx', 'gy')), may hold values from -6 to 6
- atm_pos: int32 [768], replicated, may hold values from 0 to 767, as said below
- tile_src: int32 [5120], P(('gx', 'gy')), may hold values from 0 to 767, as said below
- tile_tgt: int32 [5120], P(('gx', 'gy')), may hold values from 0 to 1
- tile_count: int32 [32], P(('gx', 'gy')), may hold values from 128 to 160, as said below
- tile_weight: bfloat16 [5120, 256, 256], P(('gx', 'gy')), may hold values from -0.0625 to 0.0625
- ocean_state: bfloat16 [128, 128, 128], P('gy', 'gx'), may hold values from -6 to 6
- land_mask: int32 [128, 128], P('gy', 'gx'), may hold values 0 or 1
- mixing: float32 [128], replicated, may hold values from 0.03 to 0.24
Outputs:
- ocean_next: bfloat16 [128, 128, 128], P('gy', 'gx')
Inputs may be any that keep to these rules, and one draw needn't show every extreme that they name: `atm_pos`: a permutation of the block positions. `tile_src`: among the 160 slots of one device, live or not, no owning device (atm_pos of the block // 24) is named by more than 8 slots; on every device with 160 live slots some owner is named by exactly 8. `tile_count`: live slots are a device's first ones; one device has exactly 160.
All inputs are finite; a program needn't handle non-finite values. No bound on the sum of `land_mask` on one device may be relied on, other than what follows from the above.
Results may differ from a plain program's by a relative error of at most 0.001.
Values may be sent and summed in bfloat16 or wider, within the bound.
A program may use at most 128 MiB of HBM per device.

v0:
```python
import jax
import jax.numpy as jnp
from jax import lax
from jax.sharding import PartitionSpec as P

RECV_SLOTS = 256


def padded(shard, sides, width, wrap):
    for axis, dim in sides:
        size, length = (lax.axis_size(axis), shard.shape[dim])
        up = [(i, (i + 1) % size) for i in range(size if wrap else size - 1)]
        down = [(j, i) for i, j in up]
        last = lax.slice_in_dim(shard, length - width, length, axis=dim)
        leading = lax.slice_in_dim(shard, 0, width, axis=dim)
        before = lax.ppermute(last, axis, up)
        after = lax.ppermute(leading, axis, down)
        shard = jnp.concatenate([before, shard, after], axis=dim)
    return shard


def partner(value, axis, distance):
    mask = 2**distance
    pairs = [(source, source ^ mask) for source in range(lax.axis_size(axis))]
    return lax.ppermute(value, axis, pairs)


def plan_tiles(sources, tile_live, atm_pos, block_count):
    positions = atm_pos[sources]
    owners = positions // block_count
    local_slot = positions % block_count
    ordinal = jnp.arange(sources.shape[0], dtype=jnp.int32)
    active = ordinal < tile_live
    earlier = (
        (owners[:, None] == owners[None, :])
        & active[None, :]
        & (ordinal[None, :] < ordinal[:, None])
    )
    order_rank = jnp.sum(earlier.astype(jnp.int32), axis=1)
    return (owners, order_rank, local_slot, active)


def local(
    atm_fields, atm_pos, tile_src, tile_tgt, tile_count, tile_weight, ocean_state, land_mask, mixing
):
    block_rows = tile_weight.shape[1]
    tiles = tile_weight.shape[0]
    channels = atm_fields.shape[1]
    block_count = atm_fields.shape[0] // block_rows
    devices = lax.axis_size("gx") * lax.axis_size("gy")
    per_peer = RECV_SLOTS // devices
    owners, order_rank, local_slot, active = plan_tiles(
        tile_src, tile_count[0], atm_pos, block_count
    )
    slots_flat = jnp.arange(RECV_SLOTS, dtype=jnp.int32)
    wanted_slot = owners * per_peer + order_rank
    matches = (wanted_slot[None, :] == slots_flat[:, None]) & active[None, :]
    asking = jnp.sum(jnp.where(matches, local_slot[None, :] + 1, 0), axis=1)
    requests = lax.all_to_all(
        asking.reshape(devices, per_peer), ("gx", "gy"), split_axis=0, concat_axis=0, tiled=True
    )
    wanted = requests.reshape(RECV_SLOTS)
    block_table = atm_fields.reshape(block_count, block_rows, channels)
    outgoing = jnp.where(
        (wanted > 0)[:, None, None],
        block_table[jnp.maximum(wanted - 1, 0)],
        jnp.zeros((), jnp.bfloat16),
    )
    outgoing = outgoing.reshape(devices, per_peer, block_rows, channels)
    arrived = lax.all_to_all(outgoing, ("gx", "gy"), split_axis=0, concat_axis=0, tiled=True)
    arrived = arrived.reshape(RECV_SLOTS, block_rows, channels)
    lat_rows = ocean_state.shape[0]
    lon_cols = ocean_state.shape[1]
    target_blocks = lat_rows * lon_cols // block_rows
    slots = jnp.where(active, owners * per_peer + order_rank, 0)
    select = (
        (tile_tgt[:, None] == jnp.arange(target_blocks, dtype=jnp.int32)[None, :]) & active[:, None]
    ).astype(jnp.float32)
    group_size = max((divisor for divisor in range(1, 33) if tiles % divisor == 0))
    groups = tiles // group_size

    def advance(running, pieces):
        weights, group_slots, group_select = pieces
        gathered = arrived[group_slots]
        partial_sum = jnp.einsum(
            "tij,tjc->tic", weights, gathered, preferred_element_type=jnp.float32
        )
        added = jnp.einsum(
            "tb,tic->bic", group_select, partial_sum, precision=lax.Precision.HIGHEST
        )
        return (running + added, None)

    starting = jnp.zeros((target_blocks, block_rows, channels), jnp.float32)
    remapped = lax.scan(
        advance,
        starting,
        (
            tile_weight.reshape(groups, group_size, block_rows, block_rows),
            slots.reshape(groups, group_size),
            select.reshape(groups, group_size, target_blocks),
        ),
    )[0]
    forcing = remapped.reshape(lat_rows, lon_cols, channels)
    mask_half = land_mask.astype(jnp.bfloat16)
    lon_state, lon_mask = (
        padded(ocean_state, (("gx", 1),), 1, True),
        padded(mask_half, (("gx", 1),), 1, True),
    )
    lat_state, lat_mask = (
        padded(ocean_state, (("gy", 0),), 1, False),
        padded(mask_half, (("gy", 0),), 1, False),
    )
    fold_state = jnp.flip(ocean_state[-1], 0)
    fold_mask = jnp.flip(mask_half[-1], 0)
    for bit_number in range(lax.axis_size("gx").bit_length() - 1):
        fold_state, fold_mask = partner((fold_state, fold_mask), "gx", bit_number)
    is_top = lax.axis_index("gy") == lax.axis_size("gy") - 1
    north_state = jnp.concatenate(
        [lat_state[2:-1], jnp.where(is_top, fold_state, lat_state[-1])[None]], axis=0
    )
    north_mask = jnp.concatenate(
        [lat_mask[2:-1], jnp.where(is_top, fold_mask, lat_mask[-1])[None]], axis=0
    )
    center = ocean_state.astype(jnp.float32)
    sides = (
        (lon_state[:, :-2], lon_mask[:, :-2]),
        (lon_state[:, 2:], lon_mask[:, 2:]),
        (lat_state[:-2], lat_mask[:-2]),
        (north_state, north_mask),
    )
    diffusion = jnp.zeros_like(center)
    for side_state, side_mask in sides:
        diffusion = diffusion + side_mask.astype(jnp.float32)[..., None] * (
            side_state.astype(jnp.float32) - center
        )
    result = mask_half.astype(jnp.float32)[..., None] * (center + forcing + mixing * diffusion)
    return result.astype(jnp.bfloat16)


def solution(mesh):
    in_specs = (
        P(("gx", "gy"), None),
        P(),
        P(("gx", "gy")),
        P(("gx", "gy")),
        P(("gx", "gy")),
        P(("gx", "gy"), None, None),
        P("gy", "gx", None),
        P("gy", "gx"),
        P(),
    )
    out_specs = P("gy", "gx", None)
    return jax.shard_map(local, mesh=mesh, in_specs=in_specs, out_specs=out_specs, check_vma=False)
```

profile of v0, /device:TPU:0, one launch (start us, length us, event | category | flops | bytes accessed | tf_op | source)
XLA Modules:
  0.0 530.6 jit_solution(13678297250485912902)
XLA Ops:
  0.0 0.8 compare_select_fusion.1
  0.8 1.9 gather_fusion.1
  3.4 0.2 convert_reduce_fusion
  3.6 0.1 select_reduce_fusion
  3.8 0.1 all_to_all.9
  3.9 14.3 %all_to_all.14 = s32[32,1,8]{2,1,0:T(1,128)S(1)} all-to-all(s32[32,1,8]{2,1,0:T(1,128)S(1)} %bitcast.58), channel_id=1, replica_groups=mesh['gx'=4,'gy'=8] {'gx','gy'}, dimensions={0} | all-to-all | bytes 2048 | tf_op jit(solution)/shard_map/all_to_all | solution.py:59
  18.2 0.1 copy.27
  18.3 0.1 reshape.189
  18.4 0.1 copy.25
  18.5 9.6 %gather_fusion.2 = bf16[256,256,128]{2,1,0:T(8,128)(2,1)} fusion(bf16[24,256,128]{2,1,0:T(8,128)(2,1)S(1)} %bitcast.54, s32[1024]{0:T(1024)S(1)} %pad_clamp_fusion.1), kind=kCustom, calls=%fused_computation.2 | custom fusion | bytes 33555456 | tf_op jit(solution)/shard_map/gather | solution.py:66
  28.1 14.0 %broadcast_select_fusion = bf16[32,8,256,128]{3,2,1,0:T(8,128)(2,1)} fusion(bf16[32,8,256,128]{3,2,1,0:T(8,128)(2,1)} %bitcast.55, pred[32,8]{1,0:T(8,128)(4,1)S(1)} %copy.25), kind=kLoop, calls=%fused_computation.18 | loop fusion | flops 8388608 | bytes 33554688 | tf_op jit(solution)/shard_map/jit(_where)/select_n | solution.py:64
  42.1 4.0 all-to-all-start.1
  46.2 3.5 collective-permute-start.4
  49.7 0.1 fusion.39
  49.7 1.7 collective-permute-start.2
  51.5 0.1 rev.8
  51.6 1.3 collective-permute-start.8
  52.9 0.1 reduce_sum.21
  53.0 0.1 div.22
  53.0 0.1 and.59
  53.1 0.1 eq.47
  53.3 87.1 %collective-permute-done = bf16[16,1]{1,0:T(8,128)(2,1)S(1)} collective-permute-done((bf16[16,1]{1,0:T(8,128)(2,1)S(1)}, bf16[16,1]{1,0:T(8,128)(2,1)S(1)}, u32[]{:S(2)}, u32[]{:S(2)}) %collective-permute-start) | collective-permute-done | bytes 64 | tf_op jit(solution)/shard_map/ppermute | solution.py:16
  140.5 1.3 collective-permute-start.11
  141.8 197.8 %collective-permute-start.5 = (bf16[1,32,128]{2,1,0:T(8,128)(2,1)S(1)}, bf16[1,32,128]{2,1,0:T(8,128)(2,1)S(1)}, u32[]{:S(2)}, u32[]{:S(2)}) collective-permute-start(bf16[1,32,128]{2,1,0:T(8,128)(2,1)S(1)} %get-tuple-element.78), channel_id=1, source_target_pairs={{0,1},{1,2},{2,3},{3,4},{4,5},{5,6},{6,7},{8,9},{9,10},{10,11},{11... | collective-permute-start | bytes 24584 | tf_op jit(solution)/shard_map/ppermute | solution.py:16
  339.6 0.9 collective-permute-start.7
  340.4 0.1 fusion.33
  340.5 2.7 collective-permute-done.7
  343.2 0.9 collective-permute-start.10
  344.1 2.8 collective-permute-done.10
  346.9 74.2 %all-to-all-done.1 = bf16[32,8,256,128]{3,2,1,0:T(8,128)(2,1)} async-done(((bf16[32,8,256,128]{3,2,1,0:T(8,128)(2,1)}), bf16[32,8,256,128]{3,2,1,0:T(8,128)(2,1)}, u32[]{:S(2)}, u32[]{:S(2)}) %all-to-all-start.1) | async-done | bytes 16777248 | tf_op jit(solution)/shard_map/all_to_all | solution.py:70
  421.2 108.0 %while.11 = (s32[]{:T(128)}, f32[2,256,128]{2,0,1:T(2,128)S(1)}, f32[5,32,2]{1,2,0:T(2,128)S(1)}, bf16[5,32,256,256]{3,2,1,0:T(8,128)(2,1)}, s32[5,32]{1,0:T(8,1...) while((s32[]{:T(128)}, f32[2,256,128]{2,0,1:T(2,128)S(1)}, ...), condition=%wide.region_3.4_spmd.clone, body=%wide.region_2.3_spmd.clone.sunk | while | flops 562168960 | bytes 19404904 | solution.py:94
  421.2 8.0 %gather_fusion = bf16[32,256,128]{2,1,0:T(8,128)(2,1)} fusion(bf16[256,256,128]{2,1,0:T(8,128)(2,1)} %get-tuple-element.148, s32[1024]{0:T(1024)S(1)} %pad_clamp_fusion.4), kind=kCustom, calls=%fused_computation.clone.clone.1 | custom fusion | bytes 4194432 | tf_op jit(solution)/shard_map/while/body/eval_jaxpr/gather | solution.py:84
  429.2 6.0 %fusion.54 = f32[32,256,128]{2,1,0:T(8,128)} fusion(bf16[32,256,128]{2,1,0:T(8,128)(2,1)} %gather_fusion, bf16[5,32,256,256]{3,2,1,0:T(8,128)(2,1)} %get-tuple-element.146, s32[]{:T(128)} %get-tuple-element.135), kind=kOutput, calls=%fused_computation.3.clone.1 | convolution fusion | flops 536870912 | bytes 10486272 | tf_op jit(solution)/shard_map/while/body/eval_jaxpr/tij,tjc->tic/dot_general | solution.py:85
  435.2 7.6 %fusion.55 = f32[2,256,128]{2,0,1:T(2,128)S(1)} fusion(f32[32,256,128]{2,1,0:T(8,128)} %fusion.54, f32[2,256,128]{2,0,1:T(2,128)S(1)} %get-tuple-element.136, pred[]{:T(512)S(6)} %compare.3, f32[5,32,2]{1,2,0:T(2,128)S(1)} %get-tuple-element.145, s32[]{:T(128)} %get-tuple-element.135), kind=kOutput, calls=%fused_computation.8.clone.1 | convolution fusion | flops 25296896 | bytes 4719621 | tf_op jit(solution)/shard_map/while/body/eval_jaxpr/tb,tic->bic/dot_general | solution.py:88
  442.8 7.9 %gather_fusion = bf16[32,256,128]{2,1,0:T(8,128)(2,1)} fusion(bf16[256,256,128]{2,1,0:T(8,128)(2,1)} %get-tuple-element.148, s32[1024]{0:T(1024)S(1)} %pad_clamp_fusion.4), kind=kCustom, calls=%fused_computation.clone.clone.1 | custom fusion | bytes 4194432 | tf_op jit(solution)/shard_map/while/body/eval_jaxpr/gather | solution.py:84
  450.8 6.0 %fusion.54 = f32[32,256,128]{2,1,0:T(8,128)} fusion(bf16[32,256,128]{2,1,0:T(8,128)(2,1)} %gather_fusion, bf16[5,32,256,256]{3,2,1,0:T(8,128)(2,1)} %get-tuple-element.146, s32[]{:T(128)} %get-tuple-element.135), kind=kOutput, calls=%fused_computation.3.clone.1 | convolution fusion | flops 536870912 | bytes 10486272 | tf_op jit(solution)/shard_map/while/body/eval_jaxpr/tij,tjc->tic/dot_general | solution.py:85
  456.8 7.6 %fusion.55 = f32[2,256,128]{2,0,1:T(2,128)S(1)} fusion(f32[32,256,128]{2,1,0:T(8,128)} %fusion.54, f32[2,256,128]{2,0,1:T(2,128)S(1)} %get-tuple-element.136, pred[]{:T(512)S(6)} %compare.3, f32[5,32,2]{1,2,0:T(2,128)S(1)} %get-tuple-element.145, s32[]{:T(128)} %get-tuple-element.135), kind=kOutput, calls=%fused_computation.8.clone.1 | convolution fusion | flops 25296896 | bytes 4719621 | tf_op jit(solution)/shard_map/while/body/eval_jaxpr/tb,tic->bic/dot_general | solution.py:88
  464.4 7.9 %gather_fusion = bf16[32,256,128]{2,1,0:T(8,128)(2,1)} fusion(bf16[256,256,128]{2,1,0:T(8,128)(2,1)} %get-tuple-element.148, s32[1024]{0:T(1024)S(1)} %pad_clamp_fusion.4), kind=kCustom, calls=%fused_computation.clone.clone.1 | custom fusion | bytes 4194432 | tf_op jit(solution)/shard_map/while/body/eval_jaxpr/gather | solution.py:84
  472.4 6.0 %fusion.54 = f32[32,256,128]{2,1,0:T(8,128)} fusion(bf16[32,256,128]{2,1,0:T(8,128)(2,1)} %gather_fusion, bf16[5,32,256,256]{3,2,1,0:T(8,128)(2,1)} %get-tuple-element.146, s32[]{:T(128)} %get-tuple-element.135), kind=kOutput, calls=%fused_computation.3.clone.1 | convolution fusion | flops 536870912 | bytes 10486272 | tf_op jit(solution)/shard_map/while/body/eval_jaxpr/tij,tjc->tic/dot_general | solution.py:85
  478.4 7.6 %fusion.55 = f32[2,256,128]{2,0,1:T(2,128)S(1)} fusion(f32[32,256,128]{2,1,0:T(8,128)} %fusion.54, f32[2,256,128]{2,0,1:T(2,128)S(1)} %get-tuple-element.136, pred[]{:T(512)S(6)} %compare.3, f32[5,32,2]{1,2,0:T(2,128)S(1)} %get-tuple-element.145, s32[]{:T(128)} %get-tuple-element.135), kind=kOutput, calls=%fused_computation.8.clone.1 | convolution fusion | flops 25296896 | bytes 4719621 | tf_op jit(solution)/shard_map/while/body/eval_jaxpr/tb,tic->bic/dot_general | solution.py:88
  486.0 7.9 %gather_fusion = bf16[32,256,128]{2,1,0:T(8,128)(2,1)} fusion(bf16[256,256,128]{2,1,0:T(8,128)(2,1)} %get-tuple-element.148, s32[1024]{0:T(1024)S(1)} %pad_clamp_fusion.4), kind=kCustom, calls=%fused_computation.clone.clone.1 | custom fusion | bytes 4194432 | tf_op jit(solution)/shard_map/while/body/eval_jaxpr/gather | solution.py:84
  493.9 6.0 %fusion.54 = f32[32,256,128]{2,1,0:T(8,128)} fusion(bf16[32,256,128]{2,1,0:T(8,128)(2,1)} %gather_fusion, bf16[5,32,256,256]{3,2,1,0:T(8,128)(2,1)} %get-tuple-element.146, s32[]{:T(128)} %get-tuple-element.135), kind=kOutput, calls=%fused_computation.3.clone.1 | convolution fusion | flops 536870912 | bytes 10486272 | tf_op jit(solution)/shard_map/while/body/eval_jaxpr/tij,tjc->tic/dot_general | solution.py:85
  500.0 7.6 %fusion.55 = f32[2,256,128]{2,0,1:T(2,128)S(1)} fusion(f32[32,256,128]{2,1,0:T(8,128)} %fusion.54, f32[2,256,128]{2,0,1:T(2,128)S(1)} %get-tuple-element.136, pred[]{:T(512)S(6)} %compare.3, f32[5,32,2]{1,2,0:T(2,128)S(1)} %get-tuple-element.145, s32[]{:T(128)} %get-tuple-element.135), kind=kOutput, calls=%fused_computation.8.clone.1 | convolution fusion | flops 25296896 | bytes 4719621 | tf_op jit(solution)/shard_map/while/body/eval_jaxpr/tb,tic->bic/dot_general | solution.py:88
  507.6 7.9 %gather_fusion = bf16[32,256,128]{2,1,0:T(8,128)(2,1)} fusion(bf16[256,256,128]{2,1,0:T(8,128)(2,1)} %get-tuple-element.148, s32[1024]{0:T(1024)S(1)} %pad_clamp_fusion.4), kind=kCustom, calls=%fused_computation.clone.clone.1 | custom fusion | bytes 4194432 | tf_op jit(solution)/shard_map/while/body/eval_jaxpr/gather | solution.py:84
  515.5 6.0 %fusion.54 = f32[32,256,128]{2,1,0:T(8,128)} fusion(bf16[32,256,128]{2,1,0:T(8,128)(2,1)} %gather_fusion, bf16[5,32,256,256]{3,2,1,0:T(8,128)(2,1)} %get-tuple-element.146, s32[]{:T(128)} %get-tuple-element.135), kind=kOutput, calls=%fused_computation.3.clone.1 | convolution fusion | flops 536870912 | bytes 10486272 | tf_op jit(solution)/shard_map/while/body/eval_jaxpr/tij,tjc->tic/dot_general | solution.py:85
  521.6 7.6 %fusion.55 = f32[2,256,128]{2,0,1:T(2,128)S(1)} fusion(f32[32,256,128]{2,1,0:T(8,128)} %fusion.54, f32[2,256,128]{2,0,1:T(2,128)S(1)} %get-tuple-element.136, pred[]{:T(512)S(6)} %compare.3, f32[5,32,2]{1,2,0:T(2,128)S(1)} %get-tuple-element.145, s32[]{:T(128)} %get-tuple-element.135), kind=kOutput, calls=%fused_computation.8.clone.1 | convolution fusion | flops 25296896 | bytes 4719621 | tf_op jit(solution)/shard_map/while/body/eval_jaxpr/tb,tic->bic/dot_general | solution.py:88
  529.3 1.1 fusion.16
  530.3 0.2 copy-done.1
  (61 shorter events, 0.4 us)
Async XLA Ops:
  0.0 18.5 %copy-start = (bf16[6144,128]{1,0:T(8,128)(2,1)S(1)}, bf16[6144,128]{1,0:T(8,128)(2,1)}, u32[]{:S(2)}) copy-start(bf16[6144,128]{1,0:T(8,128)(2,1)} %param.11) | copy-start | bytes 4718596
  42.1 4.1 copy-start.4
  42.1 11.0 %copy-start.5 = (s32[160]{0:T(256)S(1)}, s32[160]{0:T(256)}, u32[]{:S(2)}) copy-start(s32[160]{0:T(256)} %param.14) | copy-start | bytes 1924
  42.1 11.1 %copy-start.2 = (bf16[16,32,128]{2,1,0:T(8,128)(2,1)S(1)}, bf16[16,32,128]{2,1,0:T(8,128)(2,1)}, u32[]{:S(2)}) copy-start(bf16[16,32,128]{2,1,0:T(8,128)(2,1)} %param.17) | copy-start | bytes 393220
  42.1 379.1 %all-to-all-start.1 = ((bf16[32,8,256,128]{3,2,1,0:T(8,128)(2,1)}), bf16[32,8,256,128]{3,2,1,0:T(8,128)(2,1)}, u32[]{:S(2)}, u32[]{:S(2)}) async-start(bf16[32,8,256,128]{3,2,1,0:T(8,128)(2,1)} %broadcast_select_fusion), calls=%async_computation.1 | async-start | bytes 33554432 | tf_op jit(solution)/shard_map/all_to_all | solution.py:70
  46.2 95.6 %collective-permute-start.4 = (bf16[1,32]{1,0:T(2,128)(2,1)S(1)}, bf16[1,32]{1,0:T(2,128)(2,1)S(1)}, u32[]{:S(2)}, u32[]{:S(2)}) collective-permute-start(bf16[1,32]{1,0:T(2,128)(2,1)S(1)} %get-tuple-element.86), channel_id=1, source_target_pairs={{0,1},{1,2},{2,3},{3,4},{4,5},{5,6},{6,7},{8,9},{9,10},{10,11},{11... | collective-permute-start | bytes 200 | tf_op jit(solution)/shard_map/ppermute | solution.py:16
  49.7 90.7 %collective-permute-start = (bf16[16,1]{1,0:T(8,128)(2,1)S(1)}, bf16[16,1]{1,0:T(8,128)(2,1)S(1)}, u32[]{:S(2)}, u32[]{:S(2)}) collective-permute-start(bf16[16,1]{1,0:T(8,128)(2,1)S(1)} %get-tuple-element.84), channel_id=1, source_target_pairs={{0,8},{8,16},{16,24},{24,0},{1,9},{9,17},{17,25},{25,1},{2,10},{10... | collective-permute-start | bytes 104 | tf_op jit(solution)/shard_map/ppermute | solution.py:16
  49.7 90.7 %collective-permute-start.2 = (bf16[16,1]{1,0:T(8,128)(2,1)S(1)}, bf16[16,1]{1,0:T(8,128)(2,1)S(1)}, u32[]{:S(2)}, u32[]{:S(2)}) collective-permute-start(bf16[16,1]{1,0:T(8,128)(2,1)S(1)} %get-tuple-element.85), channel_id=1, source_target_pairs={{8,0},{16,8},{24,16},{0,24},{9,1},{17,9},{25,17},{1,25},{10,2},{18... | collective-permute-start | bytes 104 | tf_op jit(solution)/shard_map/ppermute | solution.py:17
  51.6 288.0 %collective-permute-start.6 = (bf16[32]{0:T(256)(128)(2,1)S(1)}, bf16[32]{0:T(256)(128)(2,1)S(1)}, u32[]{:S(2)}, u32[]{:S(2)}) collective-permute-start(bf16[32]{0:T(256)(128)(2,1)S(1)} %rev.8), channel_id=1, source_target_pairs={{0,8},{8,0},{16,24},{24,16},{1,9},{9,1},{17,25},{25,17},{2,10},{10... | collective-permute-start | bytes 200 | tf_op jit(solution)/shard_map/ppermute | solution.py:25
  51.6 288.9 %collective-permute-start.8 = (bf16[1,32]{1,0:T(2,128)(2,1)S(1)}, bf16[1,32]{1,0:T(2,128)(2,1)S(1)}, u32[]{:S(2)}, u32[]{:S(2)}) collective-permute-start(bf16[1,32]{1,0:T(2,128)(2,1)S(1)} %get-tuple-element.87), channel_id=1, source_target_pairs={{1,0},{2,1},{3,2},{4,3},{5,4},{6,5},{7,6},{9,8},{10,9},{11,10},{12... | collective-permute-start | bytes 200 | tf_op jit(solution)/shard_map/ppermute | solution.py:17
  140.5 202.8 %collective-permute-start.9 = (bf16[32,128]{1,0:T(8,128)(2,1)S(1)}, bf16[32,128]{1,0:T(8,128)(2,1)S(1)}, u32[]{:S(2)}, u32[]{:S(2)}) collective-permute-start(bf16[32,128]{1,0:T(8,128)(2,1)S(1)} %rev.9), channel_id=1, source_target_pairs={{0,8},{8,0},{16,24},{24,16},{1,9},{9,1},{17,25},{25,17},{2,10},{10... | collective-permute-start | bytes 24584 | tf_op jit(solution)/shard_map/ppermute | solution.py:25
  140.5 203.6 %collective-permute-start.11 = (bf16[1,32,128]{2,1,0:T(8,128)(2,1)S(1)}, bf16[1,32,128]{2,1,0:T(8,128)(2,1)S(1)}, u32[]{:S(2)}, u32[]{:S(2)}) collective-permute-start(bf16[1,32,128]{2,1,0:T(8,128)(2,1)S(1)} %get-tuple-element.76), channel_id=1, source_target_pairs={{1,0},{2,1},{3,2},{4,3},{5,4},{6,5},{7,6},{9,8},{10,9},{11,10},{12... | collective-permute-start | bytes 24584 | tf_op jit(solution)/shard_map/ppermute | solution.py:17
  141.8 387.4 %collective-permute-start.5 = (bf16[1,32,128]{2,1,0:T(8,128)(2,1)S(1)}, bf16[1,32,128]{2,1,0:T(8,128)(2,1)S(1)}, u32[]{:S(2)}, u32[]{:S(2)}) collective-permute-start(bf16[1,32,128]{2,1,0:T(8,128)(2,1)S(1)} %get-tuple-element.78), channel_id=1, source_target_pairs={{0,1},{1,2},{2,3},{3,4},{4,5},{5,6},{6,7},{8,9},{9,10},{10,11},{11... | collective-permute-start | bytes 24584 | tf_op jit(solution)/shard_map/ppermute | solution.py:16
  339.6 3.6 collective-permute-start.7
  340.5 188.7 %collective-permute-start.1 = (bf16[16,1,128]{2,1,0:T(2,128)(2,1)S(1)}, bf16[16,1,128]{2,1,0:T(2,128)(2,1)S(1)}, u32[]{:S(2)}, u32[]{:S(2)}) collective-permute-start(bf16[16,1,128]{2,1,0:T(2,128)(2,1)S(1)} %get-tuple-element.79), channel_id=1, source_target_pairs={{0,8},{8,16},{16,24},{24,0},{1,9},{9,17},{17,25},{25,1},{2,10},{10... | collective-permute-start | bytes 12296 | tf_op jit(solution)/shard_map/ppermute | solution.py:16
  343.2 186.0 %collective-permute-start.3 = (bf16[16,1,128]{2,1,0:T(2,128)(2,1)S(1)}, bf16[16,1,128]{2,1,0:T(2,128)(2,1)S(1)}, u32[]{:S(2)}, u32[]{:S(2)}) collective-permute-start(bf16[16,1,128]{2,1,0:T(2,128)(2,1)S(1)} %get-tuple-element.80), channel_id=1, source_target_pairs={{8,0},{16,8},{24,16},{0,24},{9,1},{17,9},{25,17},{1,25},{10,2},{18... | collective-permute-start | bytes 12296 | tf_op jit(solution)/shard_map/ppermute | solution.py:17
  343.2 3.7 collective-permute-start.10
  421.2 108.0 %copy-start.3 = (bf16[16,32,128]{2,1,0:T(8,128)(2,1)S(1)}, bf16[16,32,128]{2,1,0:T(8,128)(2,1)}, u32[]{:S(2)}) copy-start(bf16[16,32,128]{2,1,0:T(8,128)(2,1)} %param.17) | copy-start | bytes 393220
  421.2 108.1 %slice-start = ((bf16[16,32,128]{2,1,0:T(8,128)(2,1)}), bf16[15,32,128]{2,1,0:T(8,128)(2,1)S(1)}, s32[]{:S(2)}) async-start(bf16[16,32,128]{2,1,0:T(8,128)(2,1)} %param.17), calls=%async_computation.2 | async-start | bytes 245760 | tf_op jit(solution)/shard_map/slice | solution.py:119
  421.2 108.1 %copy-start.6 = (f32[128]{0:T(128)S(1)}, f32[128]{0:T(128)}, u32[]{:S(2)}) copy-start(f32[128]{0:T(128)} %param.19) | copy-start | bytes 1540
  529.2 1.4 copy-start.1
where the time goes:
time: 531 us
  starting transfers between devices  211 us (40%)
  waiting for transfers between devices  167 us (31%)
  matrix products  68.1 us (13%)
  local copies, waits for them, and re-layouts  52.5 us (10%)
  other arithmetic  16.5 us (3%)
  blocking collectives  14.3 us (3%)
    ppermute x4, starting transfers between devices, padded(): before = lax.ppermute(last, axis, up)  201 us
    ppermute x4, waiting for transfers between devices, padded(): before = lax.ppermute(last, axis, up)  87.2 us
    all_to_all x1, waiting for transfers between devices, local(): lax.all_to_all(outgoing, ('gx', 'gy'), split_axis=0, concat_axis=0, tiled...  74.2 us
    gather x5, local copies, waits for them, and re-layouts, advance(): gathered = arrived[group_slots]  39.7 us
    dot_general x5, matrix products, advance(): jnp.einsum('tb,tic->bic', group_select, partial_sum, precision=lax.Precis...  37.8 us
    dot_general x5, matrix products, advance(): jnp.einsum('tij,tjc->tic', weights, gathered, preferred_element_type=jnp....  30.2 us
    all_to_all x1, blocking collectives, local(): lax.all_to_all(asking.reshape(devices, per_peer), ('gx', 'gy'), split_axi...  14.3 us
    select_n x1, other arithmetic, local(): jnp.where((wanted > 0)[:, None, None], block_table[jnp.maximum(wanted - 1...  14 us
  transfers between devices with their start and end apart: 13, of which 4 were waited for; matrix products, arithmetic and copies ran while one was open for 20% of the time, Pallas kernels for 0%

commit v1 on v0

v1 whole, which is shorter than its diff:
```python
import functools

import jax
import jax.numpy as jnp
from jax import lax
from jax.experimental import pallas as pl
from jax.experimental.pallas import tpu as pltpu
from jax.sharding import PartitionSpec as P

RECV_SLOTS = 256
GATHER_BYTES = 64 * 2**20
MESH = pl.DeviceIdType.MESH
LOOKAHEAD = 10.0
D2D_SPEED = 10.0


def row_parts(rows):
    unit = 32
    b_rows = rows * 2 // 9 // unit * unit
    a_half = (rows - b_rows) // 2 // 16 * 16
    return {
        "B0": (0, b_rows // 2),
        "B1": (b_rows // 2, b_rows - b_rows // 2),
        "BF": (0, b_rows),
        "A0": (b_rows, a_half),
        "A1": (b_rows + a_half, rows - b_rows - a_half),
        "all": (0, rows),
    }


def pieces_of(part):
    return {"BF": ("B0", "B1"), "all": ("B0", "B1", "A0", "A1")}.get(part, (part,))


def schedule(depth, parts, rows):
    flip = {
        "x": {"o": "x", "y": "d", "x": "o", "d": "y"},
        "y": {"o": "y", "x": "d", "y": "o", "d": "x"},
    }
    messages = []
    for z in range(depth):
        for oz in range(depth):
            far = abs(oz - z)
            for part in ("A0", "A1"):
                for queue in ("x", "y"):
                    messages.append((z, queue, "o", oz, part, 2 * far + 1))
            messages.append((z, "x", "y", oz, "A1", 2 * far + 4))
            messages.append((z, "y", "x", oz, "A0", 2 * far + 4))
            for queue, step in (("up", 1), ("down", -1)):
                if 0 <= z + step < depth and (oz - z) * step <= 0:
                    for part in ("A0", "A1"):
                        messages.append((z, queue, "o", oz, part, far))
                    for across in ("o", "x", "y", "d"):
                        messages.append((z, queue, across, oz, "BF", 100 + far))
            for across in ("o", "x", "y", "d"):
                if (across, oz) == ("o", z):
                    messages.append((z, "pair", across, oz, "all", 0))
                else:
                    for part in ("BF", "A0", "A1"):
                        messages.append((z, "pair", across, oz, part, far))
        for queue in ("x", "y"):
            for part in ("B0", "B1"):
                messages.append((z, queue, "o", z, part, 0))
        messages.append((z, "x", "y", z, "B1", 2))
        messages.append((z, "y", "x", z, "B0", 2))

    arrived = {(z, "o", z, p): (0.0, None) for z in range(depth) for p in ("B0", "B1", "A0", "A1")}
    free = {}
    waiting = list(messages)
    issued = []
    while waiting:
        best = None
        for message in waiting:
            z, queue, across, oz, part, rank = message
            needs = [arrived.get((z, across, oz, p)) for p in pieces_of(part)]
            if any(n is None for n in needs):
                continue
            ready = max(n[0] for n in needs)
            start = max(ready, free.get((z, queue), 0.0))
            key = (start, rank, messages.index(message))
            if best is None or key < best[0]:
                best = (key, message, ready, start)
        _, message, ready, start = best
        waiting.remove(message)
        z, queue, across, oz, part, rank = message
        length = parts[part][1] / 256 / (D2D_SPEED if queue == "pair" else 1.0)
        end = start + length
        free[(z, queue)] = end
        if queue != "pair":
            to = z + {"up": 1, "down": -1}.get(queue, 0)
            landed = flip[queue][across] if queue in flip else across
            for p in pieces_of(part):
                arrived[(to, landed, oz, p)] = (end + 1.5, (landed, oz, part))
        issued.append((max(ready, start - LOOKAHEAD), start, z, message))
    plans = []
    for z in range(depth):
        mine = sorted((i for i in issued if i[2] == z), key=lambda i: i[:2])
        plan = []
        for _, _, _, message in mine:
            _, queue, across, oz, part, _ = message
            needs = []
            for p in pieces_of(part):
                via = arrived[(z, across, oz, p)][1]
                if via is not None and via not in needs:
                    needs.append(via)
            plan.append((queue, across, oz, part, tuple(needs), None if queue == "pair" else flip.get(queue, {}).get(across, across)))
        plans.append(plan)
    return plans


def gather_kernel(
    sizes, plans, parts, recv_index, pair_index, fields, lon, lat, out, lon_out, lat_out,
    stage, send_sem, recv_sem, pair_sem, local_sem, halo_send, halo_recv,
):
    n_gx, n_gy = sizes
    gx, gy = lax.axis_index("gx"), lax.axis_index("gy")
    rows = fields.shape[0]
    core, y, z = gx % 2, gy % 2, gy // 2
    across_x = (gx + 2) % n_gx
    across_y = gy + 1 - 2 * y
    other_core = gx + 1 - 2 * core
    right, left = (gx + 1) % n_gx, (gx + n_gx - 1) % n_gx
    north, south = (gy + 1) % n_gy, (gy + n_gy - 1) % n_gy
    mirror = n_gx - 1 - gx
    above, below = (gy + 2) % n_gy, (gy + n_gy - 2) % n_gy

    barrier = pltpu.get_barrier_semaphore()
    greeted = [
        (across_x, gy), (gx, across_y), (other_core, gy), (gx, above), (gx, below),
        (right, gy), (left, gy), (gx, north), (gx, south), (mirror, gy),
    ]
    for device in greeted:
        pl.semaphore_signal(barrier, inc=1, device_id=device, device_id_type=MESH)
    pl.semaphore_wait(barrier, len(greeted))

    take = pltpu.make_async_copy(fields, stage, local_sem.at[0])
    take.start()

    halo = []
    for i, (source, target, device) in enumerate((
        (lon.at[1], lon_out.at[0], (right, gy)),
        (lon.at[0], lon_out.at[1], (left, gy)),
        (lat.at[1], lat_out.at[0], (gx, north)),
        (lat.at[0], lat_out.at[1], (gx, south)),
        (lat.at[2], lat_out.at[2], (mirror, gy)),
    )):
        halo.append(pltpu.make_async_remote_copy(
            src_ref=source, dst_ref=target, send_sem=halo_send.at[i], recv_sem=halo_recv.at[i],
            device_id=device, device_id_type=MESH,
        ))
        halo[-1].start()

    def first_row(across, oz):
        ox = across_x if across in ("x", "d") else gx
        oy = 1 - y if across in ("y", "d") else y
        return (ox * n_gy + oz * 2 + oy) * rows

    def region(ref, across, oz, part):
        offset, length = parts[part]
        return ref.at[pl.ds(pl.multiple_of(first_row(across, oz) + offset, 16), length)]

    targets = {
        "x": (across_x, gy), "y": (gx, across_y), "pair": (other_core, gy),
        "up": (gx, above), "down": (gx, below),
    }

    def copy_of(here, entry, slot):
        queue, across, oz, part, _, landed = entry
        if (across, oz) == ("o", here):
            offset, length = parts[part]
            source = fields.at[pl.ds(offset, length)]
        else:
            source = region(out, across, oz, part)
        if queue == "pair":
            semaphore = pair_sem.at[pair_index[(across, oz, part)]]
        else:
            semaphore = recv_sem.at[recv_index[(landed, oz, part)]]
        return pltpu.make_async_remote_copy(
            src_ref=source, dst_ref=region(out, across, oz, part), send_sem=send_sem.at[slot],
            recv_sem=semaphore, device_id=targets[queue], device_id_type=MESH,
        )

    def arrival(across, oz, part, semaphore):
        place = region(out, across, oz, part)
        return pltpu.make_async_copy(place, place, semaphore)

    def arrival_pair(oz_across, oz, part):
        offset, length = parts[part]
        ox = {"x": (other_core + 2) % n_gx, "d": (other_core + 2) % n_gx}.get(oz_across, other_core)
        oy = 1 - y if oz_across in ("y", "d") else y
        start = (ox * n_gy + oz * 2 + oy) * rows + offset
        place = out.at[pl.ds(pl.multiple_of(start, 16), length)]
        return pltpu.make_async_copy(place, place, pair_sem.at[pair_index[(oz_across, oz, part)]])

    def run(here, plan):
        seen = set()
        started = []
        put = None
        for slot, entry in enumerate(plan):
            for need in entry[4]:
                if need not in seen:
                    seen.add(need)
                    arrival(*need, recv_sem.at[recv_index[need]]).wait()
            copy = copy_of(here, entry, slot)
            copy.start()
            started.append(copy)
            if slot == 8:
                take.wait()
                put = pltpu.make_async_copy(stage, region(out, "o", here, "all"), local_sem.at[1])
                put.start()
        put.wait()
        for copy in started:
            copy.wait_send()
        for entry in plan:
            if entry[0] == "pair":
                arrival_pair(entry[1], entry[2], entry[3]).wait()

    for here, plan in enumerate(plans):
        pl.when(z == here)(functools.partial(run, here, plan))
    for copy in halo:
        copy.wait()


def gather_all(fields, lon, lat, sizes):
    n_gx, n_gy = sizes
    rows, channels = fields.shape
    depth = n_gy // 2
    parts = row_parts(rows)
    plans = schedule(depth, parts, rows)
    recv_index, pair_index = {}, {}
    for here, plan in enumerate(plans):
        for queue, across, oz, part, needs, landed in plan:
            if queue == "pair":
                pair_index.setdefault((across, oz, part), len(pair_index))
            else:
                recv_index.setdefault((landed, oz, part), len(recv_index))
    slots = max(len(plan) for plan in plans)
    any_space = pl.BlockSpec(memory_space=pl.ANY)
    vmem = pl.BlockSpec(memory_space=pltpu.VMEM)
    return pl.pallas_call(
        functools.partial(gather_kernel, sizes, plans, parts, recv_index, pair_index),
        out_shape=(
            jax.ShapeDtypeStruct((rows * n_gx * n_gy, channels), fields.dtype),
            jax.ShapeDtypeStruct(lon.shape, lon.dtype),
            jax.ShapeDtypeStruct(lat.shape, lat.dtype),
        ),
        in_specs=[any_space, any_space, any_space],
        out_specs=(any_space, any_space, any_space),
        scratch_shapes=[
            pltpu.VMEM((rows, channels), fields.dtype),
            pltpu.SemaphoreType.DMA((slots,)),
            pltpu.SemaphoreType.DMA((len(recv_index),)),
            pltpu.SemaphoreType.DMA((len(pair_index),)),
            pltpu.SemaphoreType.DMA((2,)),
            pltpu.SemaphoreType.DMA((5,)),
            pltpu.SemaphoreType.DMA((5,)),
        ],
        compiler_params=pltpu.CompilerParams(
            collective_id=0, has_side_effects=True, vmem_limit_bytes=8 * 2**20
        ),
        name="gather_fields",
    )(fields, lon, lat)


def remap_kernel(
    per_step, block_of, targets, meta, weights, *refs,
):
    blocks = refs[:per_step]
    state, mask, mixing, lon, lat, out, total = refs[per_step:]
    step = pl.program_id(0)
    lat_rows, lon_cols, channels = state.shape

    @pl.when(step == 0)
    def _():
        center = state[...].astype(jnp.float32)
        wet = mask[...].astype(jnp.float32)
        west, east = lon[0].astype(jnp.float32), lon[1].astype(jnp.float32)
        top = (meta[1] != 0).astype(jnp.float32)
        inner_south = (meta[2] == 0).astype(jnp.float32)
        south = lat[0].astype(jnp.float32)
        north = lat[1].astype(jnp.float32) * (1.0 - top) + lat[2].astype(jnp.float32) * top
        south_mask = south[1] * inner_south
        sides = (
            (
                jnp.concatenate([west[0][:, None], center[:, :-1]], axis=1),
                jnp.concatenate([west[1][:, None], wet[:, :-1]], axis=1),
            ),
            (
                jnp.concatenate([center[:, 1:], east[0][:, None]], axis=1),
                jnp.concatenate([wet[:, 1:], east[1][:, None]], axis=1),
            ),
            (
                jnp.concatenate([south[0][None], center[:-1]], axis=0),
                jnp.concatenate([south_mask[None], wet[:-1]], axis=0),
            ),
            (
                jnp.concatenate([center[1:], north[0][None]], axis=0),
                jnp.concatenate([wet[1:], north[1][None]], axis=0),
            ),
        )
        diffusion = jnp.zeros_like(center)
        for side_state, side_mask in sides:
            diffusion = diffusion + side_mask * (side_state - center)
        start = center + mixing[...][0][None, None, :] * diffusion
        total[...] = start.reshape(total.shape)

    for k in range(per_step):
        tile = step * per_step + k

        @pl.when(tile < meta[0])
        def _():
            product = jnp.dot(weights[k], blocks[k][...], preferred_element_type=jnp.float32)
            total[targets[tile]] += product

    @pl.when(step == pl.num_programs(0) - 1)
    def _():
        wet = mask[...].astype(jnp.float32)
        out[...] = (wet * total[...].reshape(out.shape)).astype(out.dtype)


def remap(table, block_of, tile_tgt, meta, tile_weight, state, mask, mixing, lon, lat):
    tiles, block_rows, _ = tile_weight.shape
    channels = table.shape[1]
    cells = state.shape[0] * state.shape[1]
    per_step = max(d for d in range(1, 17) if tiles % d == 0)

    def block_spec(k):
        def index(i, block_of, tile_tgt, meta):
            return (block_of[i * per_step + k], 0)

        return pl.BlockSpec((block_rows, channels), index)

    def whole(array):
        return pl.BlockSpec(array.shape, lambda i, *_: (0,) * array.ndim)

    mixing = mixing[None]
    rest = (state, mask, mixing, lon, lat)
    return pl.pallas_call(
        functools.partial(remap_kernel, per_step),
        grid_spec=pltpu.PrefetchScalarGridSpec(
            num_scalar_prefetch=3,
            grid=(tiles // per_step,),
            in_specs=[
                pl.BlockSpec((per_step, block_rows, block_rows), lambda i, *_: (i, 0, 0)),
                *[block_spec(k) for k in range(per_step)],
                *[whole(a) for a in rest],
            ],
            out_specs=whole(state),
            scratch_shapes=[pltpu.VMEM((cells // block_rows, block_rows, channels), jnp.float32)],
        ),
        out_shape=jax.ShapeDtypeStruct(state.shape, state.dtype),
        compiler_params=pltpu.CompilerParams(
            dimension_semantics=("arbitrary",), vmem_limit_bytes=48 * 2**20
        ),
        name="remap_step",
    )(block_of, tile_tgt, meta, tile_weight, *[table] * per_step, *rest)


def exchange(atm_fields, positions, tile_live, block_rows):
    channels = atm_fields.shape[1]
    block_count = atm_fields.shape[0] // block_rows
    devices = lax.axis_size("gx") * lax.axis_size("gy")
    per_peer = RECV_SLOTS // devices
    owners = positions // block_count
    local_slot = positions % block_count
    ordinal = jnp.arange(positions.shape[0], dtype=jnp.int32)
    active = ordinal < tile_live
    earlier = (
        (owners[:, None] == owners[None, :])
        & active[None, :]
        & (ordinal[None, :] < ordinal[:, None])
    )
    wanted_slot = owners * per_peer + jnp.sum(earlier.astype(jnp.int32), axis=1)
    slots_flat = jnp.arange(RECV_SLOTS, dtype=jnp.int32)
    matches = (wanted_slot[None, :] == slots_flat[:, None]) & active[None, :]
    asking = jnp.sum(jnp.where(matches, local_slot[None, :], 0), axis=1)
    wanted = lax.all_to_all(
        asking.reshape(devices, per_peer), ("gx", "gy"), split_axis=0, concat_axis=0, tiled=True
    ).reshape(RECV_SLOTS)
    outgoing = atm_fields.reshape(block_count, block_rows, channels)[wanted]
    outgoing = outgoing.reshape(devices, per_peer, block_rows, channels)
    arrived = lax.all_to_all(outgoing, ("gx", "gy"), split_axis=0, concat_axis=0, tiled=True)
    return arrived.reshape(RECV_SLOTS * block_rows, channels), jnp.where(active, wanted_slot, 0)


def swap_edges(lon, lat, sizes):
    n_gx, n_gy = sizes

    def shift(value, axis, size, by):
        return lax.ppermute(value, axis, [(i, (i + by) % size) for i in range(size)])

    lon_out = jnp.stack([shift(lon[1], "gx", n_gx, 1), shift(lon[0], "gx", n_gx, -1)])
    fold = lax.ppermute(lat[2], "gx", [(i, n_gx - 1 - i) for i in range(n_gx)])
    lat_out = jnp.stack([shift(lat[1], "gy", n_gy, 1), shift(lat[0], "gy", n_gy, -1), fold])
    return lon_out, lat_out


def local(
    atm_fields, atm_pos, tile_src, tile_tgt, tile_count, tile_weight, ocean_state, land_mask, mixing
):
    sizes = (lax.axis_size("gx"), lax.axis_size("gy"))
    block_rows = tile_weight.shape[1]
    positions = atm_pos[tile_src]
    mask = jnp.broadcast_to(land_mask.astype(jnp.bfloat16)[..., None], ocean_state.shape)
    both = jnp.stack([ocean_state, mask])
    lon = jnp.stack([both[:, :, 0], both[:, :, -1]])
    lat = jnp.stack([both[:, 0], both[:, -1], jnp.flip(both[:, -1], 1)])
    row = lax.axis_index("gy")
    meta = jnp.stack([
        tile_count[0], (row == sizes[1] - 1).astype(jnp.int32), (row == 0).astype(jnp.int32)
    ])
    fits = atm_fields.size * 2 * sizes[0] * sizes[1] <= GATHER_BYTES
    if fits and sizes[0] == 4 and sizes[1] % 2 == 0:
        table, lon_in, lat_in = gather_all(atm_fields, lon, lat, sizes)
        block_of = positions
    else:
        table, block_of = exchange(atm_fields, positions, tile_count[0], block_rows)
        lon_in, lat_in = swap_edges(lon, lat, sizes)
    return remap(
        table, block_of, tile_tgt, meta, tile_weight, ocean_state, mask, mixing, lon_in, lat_in
    )


def solution(mesh):
    in_specs = (
        P(("gx", "gy"), None),
        P(),
        P(("gx", "gy")),
        P(("gx", "gy")),
        P(("gx", "gy")),
        P(("gx", "gy"), None, None),
        P("gy", "gx", None),
        P("gy", "gx"),
        P(),
    )
    out_specs = P("gy", "gx", None)
    return jax.shard_map(local, mesh=mesh, in_specs=in_specs, out_specs=out_specs, check_vma=False)
```

time: 531 us -> 224 us (0.42)
  Pallas kernels: 0 us -> 214 us
  starting transfers between devices: 211 us -> 0 us
  waiting for transfers between devices: 167 us -> 0 us
  matrix products: 68.1 us -> 0 us
  local copies, waits for them, and re-layouts: 52.5 us -> 5.11 us
  blocking collectives: 14.3 us -> 0 us
  other arithmetic: 16.5 us -> 3.01 us
    pallas_call x0 -> x2, Pallas kernels: none -> 214 us  [the longest x1 182 us: gather_all(): pl.pallas_call(functools.partial(gather_kernel, sizes, plans, parts, recv...]
    ppermute x12 -> x0, starting transfers between devices: 207 us -> none  [the longest x4 201 us: padded(): before = lax.ppermute(last, axis, up)]
    ppermute x12 -> x0, waiting for transfers between devices: 92.7 us -> none  [the longest x4 87.2 us: padded(): before = lax.ppermute(last, axis, up)]
    all_to_all x1 -> x0, waiting for transfers between devices: 74.2 us -> none  [local(): lax.all_to_all(outgoing, ('gx', 'gy'), split_axis=0, concat_axis=0, tiled...]
    dot_general x10 -> x0, matrix products: 68.1 us -> none  [the longest x5 37.8 us: advance(): jnp.einsum('tb,tic->bic', group_select, partial_sum, precision=lax.Precis...]
    gather x7 -> x1, local copies, waits for them, and re-layouts: 51.2 us -> 1.17 us  [local(): positions = atm_pos[tile_src]]
    all_to_all x1 -> x0, blocking collectives: 14.3 us -> none  [local(): lax.all_to_all(asking.reshape(devices, per_peer), ('gx', 'gy'), split_axi...]
    select_n x9 -> x1, other arithmetic: 14.9 us -> 0.68 us  [local(): positions = atm_pos[tile_src]]
  transfers between devices with their start and end apart: 13 -> 0, of which waited for: 4 -> 0; matrix products, arithmetic and copies ran while one was open for 20% -> 0% of each run, Pallas kernels for 0% -> 0%
where the time goes in v1:
time: 224 us; the launch traced here: 222 us
  Pallas kernels  214 us (96%)
  local copies, waits for them, and re-layouts  5.11 us (2%)
  other arithmetic  3.01 us (1%)
    pallas_call x1, Pallas kernels, gather_all(): pl.pallas_call(functools.partial(gather_kernel, sizes, plans, parts, recv...  182 us
    pallas_call x1, Pallas kernels, remap(): pl.pallas_call(functools.partial(remap_kernel, per_step), grid_spec=pltpu...  31.4 us

profile of v1, /device:TPU:0, one launch (start us, length us, event | category | flops | bytes accessed | tf_op | source)
XLA Modules:
  0.0 222.4 jit_solution(13527103130237550332)
XLA Ops:
  0.0 0.0 copy-start
  0.7 0.1 pad_add_fusion.meta
  0.7 0.7 compare_select_fusion
  1.4 0.0 copy-done
  1.4 1.2 gather_fusion
  2.6 0.7 convert_element_type.2
  3.3 0.1 stack_broadcast_in_dim.2
  3.5 0.8 pad_maximum_fusion.3
  4.3 0.7 maximum_bitcast_fusion
  5.1 0.1 broadcast_in_dim.13.refs_17_
  5.2 0.0 copy-start.2
  5.2 1.4 copy-done.2
  6.6 182.1 %gather_fields.1 = (bf16[196608,128]{1,0:T(8,128)(2,1)}, bf16[2,2,16,128]{3,2,1,0:T(8,128)(2,1)S(1)}, bf16[3,2,32,128]{3,2,1,0:T(8,128)(2,1)S(1)}) custom-call(bf16[6144,128]{1,0:T(8,128)(2,1)S(1)} %copy-done.2, bf16[2,2,16,128]{3,2,1,0:T(8,128)(2,1)S(1)} %pad_maximum_fusion.4.lon, bf16[3,2,32,128]{3,2,1,0:T(8,128)(2,1)S(1)} %pad_maximum_fusion.lat), custom_call_target="tpu_custom_call" | custom-call | tf_op jit(solution)/shard_map/gather_fields/pallas_call | solution.py:240
  188.8 0.0 copy-start.3
  188.8 0.9 copy-done.3
  189.7 0.0 copy-start.4
  189.7 0.7 copy-done.4
  190.3 0.0 copy-start.5
  190.3 0.7 copy-done.5
  191.0 0.0 copy-start.1
  191.0 31.4 %remap_step.1 = bf16[16,32,128]{2,1,0:T(8,128)(2,1)} custom-call(s32[160]{0:T(256)S(1)} %gather_fusion, s32[160]{0:T(256)S(1)} %copy-done.4, s32[3]{0:T(128)S(1)} %pad_add_fusion.meta, bf16[160,256,256]{2,1,0:T(8,128)(2,1)} %weights.1, ...), custom_call_target="tpu_custom_call" | custom-call | tf_op jit(solution)/shard_map/remap_step/pallas_call | solution.py:338
  222.4 0.0 copy-done.1
  (5 shorter events, 0.0 us)
Async XLA Ops:
  0.0 1.4 copy-start
  5.2 1.4 copy-start.2
  188.8 0.9 copy-start.3
  189.7 0.7 copy-start.4
  190.3 0.7 copy-start.5
  191.0 31.4 %copy-start.1 = (s32[768]{0:T(1024)S(1)}, s32[768]{0:T(1024)}, u32[]{:S(2)}) copy-start(s32[768]{0:T(1024)} %param.10) | copy-start | bytes 9220

commit v2 on v1

--- a/solution.py
+++ b/solution.py
@@ -9,6 +9,7 @@
 
 RECV_SLOTS = 256
 GATHER_BYTES = 64 * 2**20
+VMEM_BYTES = 67043328
 MESH = pl.DeviceIdType.MESH
 LOOKAHEAD = 10.0
 D2D_SPEED = 10.0
@@ -109,7 +110,8 @@
 
 
 def gather_kernel(
-    sizes, plans, parts, recv_index, pair_index, fields, lon, lat, out, lon_out, lat_out,
+    sizes, plans, parts, recv_index, pair_index, fields, lon, lat, weights, out, lon_out, lat_out,
+    weights_out,
     stage, send_sem, recv_sem, pair_sem, local_sem, halo_send, halo_recv,
 ):
     n_gx, n_gy = sizes
@@ -135,6 +137,8 @@
 
     take = pltpu.make_async_copy(fields, stage, local_sem.at[0])
     take.start()
+    near = pltpu.make_async_copy(weights, weights_out, local_sem.at[2])
+    near.start()
 
     halo = []
     for i, (source, target, device) in enumerate((
@@ -219,9 +223,10 @@
         pl.when(z == here)(functools.partial(run, here, plan))
     for copy in halo:
         copy.wait()
-
-
-def gather_all(fields, lon, lat, sizes):
+    near.wait()
+
+
+def gather_all(fields, lon, lat, weights, sizes):
     n_gx, n_gy = sizes
     rows, channels = fields.shape
     depth = n_gy // 2
@@ -235,48 +240,71 @@
             else:
                 recv_index.setdefault((landed, oz, part), len(recv_index))
     slots = max(len(plan) for plan in plans)
+    grant = max(VMEM_BYTES - weights.size * 2 - 12 * 2**20, 8 * 2**20)
     any_space = pl.BlockSpec(memory_space=pl.ANY)
-    vmem = pl.BlockSpec(memory_space=pltpu.VMEM)
+    hbm = pl.BlockSpec(memory_space=pltpu.HBM)
     return pl.pallas_call(
         functools.partial(gather_kernel, sizes, plans, parts, recv_index, pair_index),
         out_shape=(
             jax.ShapeDtypeStruct((rows * n_gx * n_gy, channels), fields.dtype),
             jax.ShapeDtypeStruct(lon.shape, lon.dtype),
             jax.ShapeDtypeStruct(lat.shape, lat.dtype),
+            jax.ShapeDtypeStruct(weights.shape, weights.dtype),
         ),
-        in_specs=[any_space, any_space, any_space],
-        out_specs=(any_space, any_space, any_space),
+        in_specs=[hbm, any_space, any_space, hbm],
+        out_specs=(hbm, any_space, any_space, any_space),
         scratch_shapes=[
             pltpu.VMEM((rows, channels), fields.dtype),
             pltpu.SemaphoreType.DMA((slots,)),
             pltpu.SemaphoreType.DMA((len(recv_index),)),
             pltpu.SemaphoreType.DMA((len(pair_index),)),
-            pltpu.SemaphoreType.DMA((2,)),
+            pltpu.SemaphoreType.DMA((3,)),
             pltpu.SemaphoreType.DMA((5,)),
             pltpu.SemaphoreType.DMA((5,)),
         ],
         compiler_params=pltpu.CompilerParams(
-            collective_id=0, has_side_effects=True, vmem_limit_bytes=8 * 2**20
+            collective_id=0, has_side_effects=True, vmem_limit_bytes=grant
+        ),
+        cost_estimate=pl.CostEstimate(
+            flops=0, transcendentals=0, bytes_accessed=10 * rows * channels * 2 * n_gx * n_gy
         ),
         name="gather_fields",
-    )(fields, lon, lat)
+    )(fields, lon, lat, weights)
 
 
 def remap_kernel(
-    per_step, block_of, targets, meta, weights, *refs,
+    per_step, place_of, source, targets, live, weights, *refs,
 ):
     blocks = refs[:per_step]
-    state, mask, mixing, lon, lat, out, total = refs[per_step:]
+    state, mask, mixing, lon, lat, out, base, total = refs[per_step:]
     step = pl.program_id(0)
     lat_rows, lon_cols, channels = state.shape
+    block_rows = weights.shape[1]
+    target_blocks = total.shape[1] // channels
+
+    columns = []
+    for k in range(per_step):
+        tile = step * per_step + k
+        target = jnp.where(tile < live[0], targets[tile], -1)
+        block = blocks[k][...]
+        columns.append(jnp.concatenate(
+            [jnp.where(target == b, block, jnp.zeros_like(block)) for b in range(target_blocks)],
+            axis=1,
+        ))
+    product = jnp.dot(
+        jnp.concatenate([weights[k] for k in range(per_step)], axis=1),
+        jnp.concatenate(columns, axis=0),
+        preferred_element_type=jnp.float32,
+    )
 
     @pl.when(step == 0)
     def _():
         center = state[...].astype(jnp.float32)
         wet = mask[...].astype(jnp.float32)
+        row = lax.axis_index("gy")
+        top = (row == lax.axis_size("gy") - 1).astype(jnp.float32)
+        inner_south = (row != 0).astype(jnp.float32)
         west, east = lon[0].astype(jnp.float32), lon[1].astype(jnp.float32)
-        top = (meta[1] != 0).astype(jnp.float32)
-        inner_south = (meta[2] == 0).astype(jnp.float32)
         south = lat[0].astype(jnp.float32)
         north = lat[1].astype(jnp.float32) * (1.0 - top) + lat[2].astype(jnp.float32) * top
         south_mask = south[1] * inner_south
@@ -301,44 +329,42 @@
         diffusion = jnp.zeros_like(center)
         for side_state, side_mask in sides:
             diffusion = diffusion + side_mask * (side_state - center)
-        start = center + mixing[...][0][None, None, :] * diffusion
-        total[...] = start.reshape(total.shape)
-
-    for k in range(per_step):
-        tile = step * per_step + k
-
-        @pl.when(tile < meta[0])
-        def _():
-            product = jnp.dot(weights[k], blocks[k][...], preferred_element_type=jnp.float32)
-            total[targets[tile]] += product
+        base[...] = (center + mixing[...][0][None, None, :] * diffusion).reshape(base.shape)
+        total[...] = product
+
+    @pl.when(step != 0)
+    def _():
+        total[...] += product
 
     @pl.when(step == pl.num_programs(0) - 1)
     def _():
+        forcing = jnp.concatenate(
+            [total[:, b * channels:(b + 1) * channels] for b in range(target_blocks)], axis=0
+        )
         wet = mask[...].astype(jnp.float32)
-        out[...] = (wet * total[...].reshape(out.shape)).astype(out.dtype)
-
-
-def remap(table, block_of, tile_tgt, meta, tile_weight, state, mask, mixing, lon, lat):
+        out[...] = (wet * (base[...] + forcing).reshape(out.shape)).astype(out.dtype)
+
+
+def remap(table, place_of, source, tile_tgt, live, tile_weight, state, mask, mixing, lon, lat):
     tiles, block_rows, _ = tile_weight.shape
     channels = table.shape[1]
     cells = state.shape[0] * state.shape[1]
     per_step = max(d for d in range(1, 17) if tiles % d == 0)
 
     def block_spec(k):
-        def index(i, block_of, tile_tgt, meta):
-            return (block_of[i * per_step + k], 0)
+        def index(i, place_of, source, tile_tgt, live):
+            return (place_of[source[i * per_step + k]], 0)
 
         return pl.BlockSpec((block_rows, channels), index)
 
     def whole(array):
         return pl.BlockSpec(array.shape, lambda i, *_: (0,) * array.ndim)
 
-    mixing = mixing[None]
-    rest = (state, mask, mixing, lon, lat)
+    rest = (state, mask, mixing[None], lon, lat)
     return pl.pallas_call(
         functools.partial(remap_kernel, per_step),
         grid_spec=pltpu.PrefetchScalarGridSpec(
-            num_scalar_prefetch=3,
+            num_scalar_prefetch=4,
             grid=(tiles // per_step,),
             in_specs=[
                 pl.BlockSpec((per_step, block_rows, block_rows), lambda i, *_: (i, 0, 0)),
@@ -346,14 +372,17 @@
                 *[whole(a) for a in rest],
             ],
             out_specs=whole(state),
-            scratch_shapes=[pltpu.VMEM((cells // block_rows, block_rows, channels), jnp.float32)],
+            scratch_shapes=[
+                pltpu.VMEM((cells, channels), jnp.float32),
+                pltpu.VMEM((block_rows, cells // block_rows * channels), jnp.float32),
+            ],
         ),
         out_shape=jax.ShapeDtypeStruct(state.shape, state.dtype),
         compiler_params=pltpu.CompilerParams(
-            dimension_semantics=("arbitrary",), vmem_limit_bytes=48 * 2**20
+            dimension_semantics=("arbitrary",), vmem_limit_bytes=20 * 2**20
         ),
         name="remap_step",
-    )(block_of, tile_tgt, meta, tile_weight, *[table] * per_step, *rest)
+    )(place_of, source, tile_tgt, live, tile_weight, *[table] * per_step, *rest)
 
 
 def exchange(atm_fields, positions, tile_live, block_rows):
@@ -400,24 +429,21 @@
 ):
     sizes = (lax.axis_size("gx"), lax.axis_size("gy"))
     block_rows = tile_weight.shape[1]
-    positions = atm_pos[tile_src]
     mask = jnp.broadcast_to(land_mask.astype(jnp.bfloat16)[..., None], ocean_state.shape)
     both = jnp.stack([ocean_state, mask])
     lon = jnp.stack([both[:, :, 0], both[:, :, -1]])
     lat = jnp.stack([both[:, 0], both[:, -1], jnp.flip(both[:, -1], 1)])
-    row = lax.axis_index("gy")
-    meta = jnp.stack([
-        tile_count[0], (row == sizes[1] - 1).astype(jnp.int32), (row == 0).astype(jnp.int32)
-    ])
     fits = atm_fields.size * 2 * sizes[0] * sizes[1] <= GATHER_BYTES
     if fits and sizes[0] == 4 and sizes[1] % 2 == 0:
-        table, lon_in, lat_in = gather_all(atm_fields, lon, lat, sizes)
-        block_of = positions
+        table, lon_in, lat_in, tile_weight = gather_all(atm_fields, lon, lat, tile_weight, sizes)
+        place_of, source = atm_pos, tile_src
     else:
-        table, block_of = exchange(atm_fields, positions, tile_count[0], block_rows)
+        table, place_of = exchange(atm_fields, atm_pos[tile_src], tile_count[0], block_rows)
+        source = jnp.arange(tile_src.shape[0], dtype=jnp.int32)
         lon_in, lat_in = swap_edges(lon, lat, sizes)
     return remap(
-        table, block_of, tile_tgt, meta, tile_weight, ocean_state, mask, mixing, lon_in, lat_in
+        table, place_of, source, tile_tgt, tile_count, tile_weight, ocean_state, mask, mixing,
+        lon_in, lat_in,
     )
 
 

time: 224 us -> 201 us (0.90)
  Pallas kernels: 214 us -> 196 us
  local copies, waits for them, and re-layouts: 5.11 us -> 1.71 us
    pallas_call x1, Pallas kernels: 31.4 us -> 13.4 us  [remap(): pl.pallas_call(functools.partial(remap_kernel, per_step), grid_spec=pltpu...]
where the time goes in v2:
time: 201 us; the launch traced here: 200 us
  Pallas kernels  196 us (98%)
  other arithmetic  2.24 us (1%)
    pallas_call x1, Pallas kernels, gather_all(): pl.pallas_call(functools.partial(gather_kernel, sizes, plans, parts, recv...  182 us
    pallas_call x1, Pallas kernels, remap(): pl.pallas_call(functools.partial(remap_kernel, per_step), grid_spec=pltpu...  13.4 us

profile of v2, /device:TPU:0, one launch (start us, length us, event | category | flops | bytes accessed | tf_op | source)
XLA Modules:
  0.0 200.3 jit_solution(2946754736512486521)
XLA Ops:
  0.0 0.0 copy-start.1
  0.0 0.0 copy-start.5
  0.0 0.0 copy-start.4
  0.0 0.0 copy-start.3
  0.0 0.0 copy-start.2
  0.7 0.7 convert_element_type.3
  1.4 0.1 stack_broadcast_in_dim.2
  1.5 0.8 pad_maximum_fusion.3
  2.4 0.7 maximum_bitcast_fusion
  3.1 0.1 broadcast_in_dim.4.refs_17_
  3.3 0.0 copy-start
  3.3 1.4 copy-done
  4.7 182.2 %gather_fields.1 = (bf16[196608,128]{1,0:T(8,128)(2,1)}, bf16[2,2,16,128]{3,2,1,0:T(8,128)(2,1)S(1)}, bf16[3,2,32,128]{3,2,1,0:T(8,128)(2,1)S(1)}, bf16[160,256,256]{2,1,0:T(8,128)(2,1)S(1)}) custom-call(bf16[6144,128]{1,0:T(8,128)(2,1)S(1)} %copy-done, bf16[2,2,16,128]{3,2,1,0:T(8,128)(2,1)S(1)} %pad_maximum_fusion.4.lon, ...), custom_call_target="tpu_custom_call" | custom-call | bytes 503316480 | tf_op jit(solution)/shard_map/gather_fields/pallas_call | solution.py:246
  186.9 0.0 copy-done.1
  186.9 0.0 copy-done.5
  186.9 0.0 copy-done.4
  186.9 0.0 copy-done.3
  186.9 0.0 copy-done.2
  186.9 13.4 %remap_step.1 = bf16[16,32,128]{2,1,0:T(8,128)(2,1)} custom-call(s32[768]{0:T(1024)S(1)} %copy-done.2, s32[160]{0:T(256)S(1)} %copy-done.3, s32[160]{0:T(256)S(1)} %copy-done.4, s32[1]{0:T(128)S(6)} %copy.19.live, bf16[160,256,256]{2,1,0:T(8,128)(2,1)S(1)} %get-tuple-element.9.weights, ...), custom_call_target="tpu_custom_call" | custom-call | tf_op jit(solution)/shard_map/remap_step/pallas_call | solution.py:364
  (4 shorter events, 0.0 us)
Async XLA Ops:
  0.0 186.9 %copy-start.1 = (bf16[16,32,128]{2,1,0:T(8,128)(2,1)S(1)}, bf16[16,32,128]{2,1,0:T(8,128)(2,1)}, u32[]{:S(2)}) copy-start(bf16[16,32,128]{2,1,0:T(8,128)(2,1)} %refs_16_.1) | copy-start | bytes 393220
  0.0 186.9 %copy-start.5 = (f32[128]{0:T(128)S(1)}, f32[128]{0:T(128)}, u32[]{:S(2)}) copy-start(f32[128]{0:T(128)} %param.17) | copy-start | bytes 1540
  0.0 186.9 %copy-start.4 = (s32[160]{0:T(256)S(1)}, s32[160]{0:T(256)}, u32[]{:S(2)}) copy-start(s32[160]{0:T(256)} %targets.1) | copy-start | bytes 1924
  0.0 186.9 %copy-start.3 = (s32[160]{0:T(256)S(1)}, s32[160]{0:T(256)}, u32[]{:S(2)}) copy-start(s32[160]{0:T(256)} %source.1) | copy-start | bytes 1924
  0.0 186.9 %copy-start.2 = (s32[768]{0:T(1024)S(1)}, s32[768]{0:T(1024)}, u32[]{:S(2)}) copy-start(s32[768]{0:T(1024)} %place_of.1) | copy-start | bytes 9220
  3.3 1.4 copy-start
